TPU v7x, 32 devices: a whole 2x2x4 slice. The times are simulated.
32 devices in a mesh: groups: 2 (over y), expert: 8 (over z, x), tensor: 2 (over core).
Axes of the slice: x: 2, y: 2, z: 4, core: 2. Of those that a mesh axis runs over, the one named last changes fastest.
Arguments:
- tokens: bfloat16 [1024, 1536], P(('groups', 'expert')), parts along dimension 0, may hold values from -12 to 12
- gain: float32 [1536], replicated, may hold values from 0.25 to 1.75
- route_ids: int32 [1024, 4], P(('groups', 'expert')), parts along dimension 0, may hold values from 0 to 3, as said below
- route_weights: float32 [1024, 4], P(('groups', 'expert')), parts along dimension 0, may hold values from 0.05 to 0.5
- w_gate: bfloat16 [8, 1536, 768], P('expert', None, 'tensor'), may hold values from -0.15625 to 0.15625
- w_up: bfloat16 [8, 1536, 768], P('expert', None, 'tensor'), may hold values from -0.15625 to 0.15625
- w_down: bfloat16 [8, 768, 1536], P('expert', 'tensor'), may hold values from -0.15625 to 0.15625
Outputs:
- mixed: bfloat16 [1024, 1536], P(('groups', 'expert')), parts along dimension 0
There are 2 independent parts, one for each index of `groups`. A program takes and returns all parts, laid end to end along the dimension named above; an argument that names none is the same for every part. Nothing has to cross between parts.
Inputs may be any that keep to these rules, and one draw needn't show every extreme that they name: `route_ids`: each row names 4 different experts. In each aligned block of 32 rows no expert is named more than 32 times; one expert, the same in every block, is named exactly 32 times in every block, and the other experts' counts within a block differ by at most one.
All inputs are finite; a program needn't handle non-finite values.
Results may differ from a plain program's by a relative error of at most 0.0045.
Values may be sent and summed in bfloat16 or wider, within the bound.
A program may use at most 64 MiB of HBM per device.

v0:
```python
import jax
import jax.numpy as jnp
from jax import lax
from jax.sharding import PartitionSpec as P


def gated_unit(gate_val, up_val):
    return gate_val * jax.nn.sigmoid(1.702 * gate_val) * (up_val + 1.0)


def route_tables(chosen_ids, chosen_weights, expert_count, slot_room):
    row_count, top_count = chosen_ids.shape
    matches = (chosen_ids[:, :, None] == jnp.arange(expert_count, dtype=jnp.int32)).astype(
        jnp.float32
    )
    flat_match = matches.reshape(row_count * top_count, expert_count)
    order_range = jnp.arange(row_count * top_count, dtype=jnp.int32)
    earlier = (order_range[:, None] > order_range[None, :]).astype(jnp.float32)
    before = jnp.dot(
        earlier, flat_match, precision=lax.Precision.HIGHEST, preferred_element_type=jnp.float32
    )
    position = jnp.sum(before * flat_match, axis=1).reshape(row_count, top_count).astype(jnp.int32)
    slot_index = chosen_ids * slot_room + position
    targets = jnp.arange(expert_count * slot_room, dtype=jnp.int32)
    slot_hits = slot_index[None, :, :] == targets[:, None, None]
    send_table = jnp.sum(slot_hits.astype(jnp.float32), axis=2).astype(jnp.bfloat16)
    mix_table = jnp.sum(jnp.where(slot_hits, chosen_weights[None, :, :], 0.0), axis=2)
    return (send_table, mix_table)


def per_device(tokens, gain, route_ids, route_weights, w_gate, w_up, w_down):
    expert_axis = lax.axis_size("expert")
    expert_count = expert_axis // 2
    tensor_count = lax.axis_size("tensor")
    own_rows = tokens.shape[0] // tensor_count
    top_count = route_ids.shape[1]
    capacity = max(2, own_rows * top_count // expert_count)
    gate_local = w_gate[0]
    up_local = w_up[0]
    down_local = w_down[0]
    first_row = lax.axis_index("tensor") * own_rows
    own_tokens = lax.dynamic_slice_in_dim(tokens, first_row, own_rows, 0)
    own_ids = lax.dynamic_slice_in_dim(route_ids, first_row, own_rows, 0)
    own_weights = lax.dynamic_slice_in_dim(route_weights, first_row, own_rows, 0)
    resident = own_tokens.astype(jnp.float32)
    inv_rms = lax.rsqrt(jnp.mean(resident * resident, axis=1, keepdims=True) + 1e-05)
    normed = (resident * inv_rms * gain).astype(jnp.bfloat16)
    send_table, mix_table = route_tables(own_ids, own_weights, expert_count, capacity)
    packed = jnp.dot(send_table, normed, preferred_element_type=jnp.float32).astype(jnp.bfloat16)
    features = packed.shape[1]
    by_expert = packed.reshape(expert_count, 1, capacity, features)
    outgoing = jnp.broadcast_to(by_expert, (expert_count, 2, capacity, features)).reshape(
        expert_axis * capacity, features
    )
    arrived = lax.all_to_all(outgoing, "expert", split_axis=0, concat_axis=0, tiled=True)
    row_piece = lax.all_gather(arrived, "tensor", axis=0, tiled=True)
    gate_val = jnp.dot(row_piece, gate_local, preferred_element_type=jnp.float32)
    up_val = jnp.dot(row_piece, up_local, preferred_element_type=jnp.float32)
    hidden = gated_unit(gate_val, up_val).astype(jnp.bfloat16)
    partial_value = lax.psum_scatter(
        jnp.dot(hidden, down_local, preferred_element_type=jnp.float32),
        "tensor",
        scatter_dimension=0,
        tiled=True,
    )
    returned = lax.all_to_all(
        partial_value.astype(jnp.bfloat16), "expert", split_axis=0, concat_axis=0, tiled=True
    ).astype(partial_value.dtype)
    expert_out = (
        returned.reshape(expert_count, 2, capacity, features)
        .sum(axis=1)
        .reshape(expert_count * capacity, features)
    )
    weighted = jnp.dot(
        mix_table.T, expert_out, precision=lax.Precision.HIGHEST, preferred_element_type=jnp.float32
    )
    finished = (resident + weighted).astype(jnp.bfloat16)
    return lax.all_gather(finished, "tensor", axis=0, tiled=True)


def solution(mesh):
    placed = (
        P(("groups", "expert"), None),
        P(),
        P(("groups", "expert"), None),
        P(("groups", "expert"), None),
        P("expert", None, "tensor"),
        P("expert", None, "tensor"),
        P("expert", "tensor", None),
    )
    return jax.shard_map(
        per_device,
        mesh=mesh,
        in_specs=placed,
        out_specs=P(("groups", "expert"), None),
        check_vma=False,
    )
```

profile of v0, /device:TPU:0, one launch (start us, length us, event | category | flops | bytes accessed | tf_op | source)
XLA Modules:
  0.0 106.2 jit_solution(7419597730249863763)
XLA Ops:
  6.5 0.0 copy-start
  6.5 0.0 all-gather.2.cloned.1.call-start
  6.5 1.1 %fusion.18 = f32[32]{0:T(128)S(1)} fusion(bf16[64,1536]{1,0:T(8,128)(2,1)} %param.7, s32[]{:T(128)S(6)} %select_n.9), kind=kLoop, calls=%fused_computation.24 | loop fusion | flops 147424 | bytes 98436 | tf_op jit(solution)/shard_map/reduce_sum | solution.py:46
  7.7 0.8 constant_dynamic-slice_fusion.1
  8.4 0.8 constant_dynamic-slice_fusion
  9.2 0.1 copy.14
  9.3 0.1 eq.30
  9.4 0.1 fusion.9
  9.5 0.1 convert_element_type.42
  9.7 0.1 copy.13
  9.7 0.1 convert_reduce_fusion.1
  9.9 1.2 %convolution_convert_fusion = bf16[128,1536]{1,0:T(8,128)(2,1)S(1)} fusion(f32[1536]{0:T(1024)} %param.8, f32[32]{0:T(128)S(1)} %add_rsqrt_fusion, bf16[64,1536]{1,0:T(8,128)(2,1)} %param.7, s32[]{:T(128)S(6)} %select_n.9, bf16[128,32]{0,1:T(8,128)(2,1)S(1)} %get-tuple-element.5), kind=kOutput, calls=%fused_computation | convolution fusion | flops 12976128 | bytes 508036 | tf_op jit(solution)/shard_map/dot_general | solution.py:49
  11.1 0.1 broadcast_in_dim.19
  11.2 27.3 %all_to_all.21 = bf16[8,32,1536]{2,1,0:T(8,128)(2,1)} all-to-all(bf16[8,32,1536]{2,1,0:T(8,128)(2,1)S(1)} %bitcast.25), channel_id=1, replica_groups=mesh['groups'=2,'expert'=8,'tensor'=2] {'expert'}, dimensions={0} | all-to-all | bytes 1572864 | tf_op jit(solution)/shard_map/all_to_all | solution.py:55
  38.5 0.0 all-gather.2.cloned.1.call-update
  38.5 0.0 reduce-scatter.2.cloned.1.call-start
  38.6 9.0 %all-gather.2.cloned.1.call-done = bf16[512,1536]{1,0:T(8,128)(2,1)} async-done(((bf16[256,1536]{1,0:T(8,128)(2,1)}), bf16[512,1536]{1,0:T(8,128)(2,1)}) %all-gather.2.cloned.1.call-update) | async-done | bytes 1572880 | tf_op jit(solution)/shard_map/all_gather | solution.py:56
  47.5 0.0 copy-start.2
  47.5 2.8 %fusion.7 = f32[512,384]{1,0:T(8,128)S(1)} fusion(bf16[512,1536]{1,0:T(8,128)(2,1)} %all-gather.2.cloned.1.call-done, bf16[1,1536,384]{2,1,0:T(8,128)(2,1)} %param.11), kind=kOutput, calls=%fused_computation.10 | convolution fusion | flops 603979776 | bytes 3538944 | tf_op jit(solution)/shard_map/dot_general | solution.py:57
  50.4 0.0 copy-done
  50.4 0.0 copy-done.2
  50.4 4.8 %fusion.3 = f32[512,1536]{1,0:T(8,128)} fusion(bf16[512,1536]{1,0:T(8,128)(2,1)S(1)} %copy-done.2, bf16[1,384,1536]{2,1,0:T(8,128)(2,1)S(1)} %copy-done, bf16[1,1536,384]{2,1,0:T(8,128)(2,1)} %param.12, f32[512,384]{1,0:T(8,128)S(1)} %fusion.7), kind=kOutput, calls=%fused_computation.7 | convolution fusion | flops 1209532416 | bytes 7864320 | tf_op jit(solution)/shard_map/dot_general | solution.py:61
  55.1 0.0 reduce-scatter.2.cloned.1.call-update
  55.2 12.5 %reduce-scatter.2.cloned.1.call-done = f32[256,1536]{1,0:T(8,128)} async-done(((f32[512,1536]{1,0:T(8,128)}), f32[256,1536]{1,0:T(8,128)}) %reduce-scatter.2.cloned.1.call-update) | async-done | bytes 1572880 | tf_op jit(solution)/shard_map/reduce_scatter | solution.py:60
  67.7 1.5 %convert_element_type.48 = bf16[256,1536]{1,0:T(8,128)(2,1)S(1)} convert(f32[256,1536]{1,0:T(8,128)} %reduce-scatter.2.cloned.1.call-done) | non-fusion elementwise | flops 393216 | bytes 2359296 | tf_op jit(solution)/shard_map/convert_element_type | solution.py:67
  69.1 26.1 %all_to_all.22 = bf16[8,32,1536]{2,1,0:T(8,128)(2,1)S(1)} all-to-all(bf16[8,32,1536]{2,1,0:T(8,128)(2,1)S(1)} %bitcast.26), channel_id=1, replica_groups=mesh['groups'=2,'expert'=8,'tensor'=2] {'expert'}, dimensions={0} | all-to-all | bytes 1572864 | tf_op jit(solution)/shard_map/all_to_all | solution.py:66
  95.3 0.0 copy-start.1
  95.3 0.1 convert_reduce_fusion
  95.4 0.8 copy-done.1
  96.2 0.5 fusion
  96.7 1.9 %all_gather.7 = bf16[64,1536]{1,0:T(8,128)(2,1)S(1)} all-gather(bf16[32,1536]{1,0:T(8,128)(2,1)S(1)} %fusion), channel_id=1, replica_groups=mesh['groups'=2,'expert'=8,'tensor'=2] {'tensor'}, dimensions={0}, use_global_device_ids=true | all-gather | bytes 294912 | tf_op jit(solution)/shard_map/all_gather | solution.py:78
  98.7 0.7 copy.16
  (3 shorter events, 0.0 us)
Async XLA Ops:
  6.5 43.8 %copy-start = (bf16[1,384,1536]{2,1,0:T(8,128)(2,1)S(1)}, bf16[1,384,1536]{2,1,0:T(8,128)(2,1)}, u32[]{:S(2)}) copy-start(bf16[1,384,1536]{2,1,0:T(8,128)(2,1)} %param.13) | copy-start | bytes 3538948
  6.5 41.0 %all-gather.2.cloned.1.call-start = ((), (), s32[]{:S(2)}) async-start(), calls=%async_computation.3 | async-start | bytes 2359296 | tf_op jit(solution)/shard_map/all_gather | solution.py:56
  38.5 29.1 %reduce-scatter.2.cloned.1.call-start = ((), (), s32[]{:S(2)}) async-start(), calls=%async_computation.4 | async-start | bytes 4718592 | tf_op jit(solution)/shard_map/reduce_scatter | solution.py:60
  47.5 2.9 %copy-start.2 = (bf16[512,1536]{1,0:T(8,128)(2,1)S(1)}, bf16[512,1536]{1,0:T(8,128)(2,1)}, u32[]{:S(2)}) copy-start(bf16[512,1536]{1,0:T(8,128)(2,1)} %all-gather.2.cloned.1.call-done) | copy-start | bytes 4718596
  95.3 0.9 copy-start.1
Sparse Core Ops, SparseCore 0:
  38.6 8.8 all-gather.1
  55.3 12.3 reduce-scatter.1
where the time goes:
time: 107 us; the launch traced here: 106 us
  blocking collectives  55.4 us (52%)
  waiting for transfers between devices  21.5 us (20%)
  between operations  13.5 us (13%)
  matrix products  9.5 us (9%)
  local copies, waits for them, and re-layouts  3.43 us (3%)
  other arithmetic  2.86 us (3%)
    all_to_all x1, blocking collectives, per_device(): lax.all_to_all(outgoing, 'expert', split_axis=0, concat_axis=0, tiled=True)  27.3 us
    all_to_all x1, blocking collectives, per_device(): lax.all_to_all(partial_value.astype(jnp.bfloat16), 'expert', split_axis=0...  26.1 us
    reduce_scatter x1, waiting for transfers between devices, per_device(): lax.psum_scatter(jnp.dot(hidden, down_local, preferred_element_type=jnp.f...  12.5 us
    all_gather x1, waiting for transfers between devices, per_device(): row_piece = lax.all_gather(arrived, 'tensor', axis=0, tiled=True)  8.95 us
    dot_general x1, matrix products, per_device(): jnp.dot(hidden, down_local, preferred_element_type=jnp.float32)  4.78 us
    dot_general x1, matrix products, per_device(): jnp.dot(row_piece, gate_local, preferred_element_type=jnp.float32)  2.83 us
  transfers between devices with their start and end apart: 2, of which 2 were waited for; matrix products, arithmetic and copies ran while one was open for 0% of the time, Pallas kernels for 0%

commit v1 on v0

--- a/solution.py
+++ b/solution.py
@@ -1,11 +1,230 @@
+import functools
+
 import jax
 import jax.numpy as jnp
 from jax import lax
+from jax.experimental import pallas as pl
+from jax.experimental.pallas import tpu as pltpu
 from jax.sharding import PartitionSpec as P
+
+MESH = pl.DeviceIdType.MESH
 
 
 def gated_unit(gate_val, up_val):
     return gate_val * jax.nn.sigmoid(1.702 * gate_val) * (up_val + 1.0)
+
+
+def flipped(index, bits, count):
+    out = index
+    power = 1
+    while power < count:
+        if bits // power % 2:
+            out = out + power - 2 * power * lax.rem(index // power, 2)
+        power *= 2
+    return out
+
+
+def dense_kernel(
+    experts,
+    tokens_ref,
+    gain_ref,
+    ids_ref,
+    weights_ref,
+    gate_ref,
+    up_ref,
+    down_ref,
+    out_ref,
+    wg,
+    wu,
+    wd,
+    xa,
+    xb,
+    own_out,
+    x_send,
+    x_recv,
+    z_send,
+    z_recv,
+    final,
+    load_sem,
+    swap_send,
+    swap_recv,
+    xa_send,
+    xa_recv,
+    xb_send,
+    xb_recv,
+    px_send,
+    px_recv,
+    pz_send,
+    pz_recv,
+    last_send,
+    last_recv,
+):
+    me = lax.axis_index("expert")
+    core = lax.axis_index("tensor")
+    place = me // 2
+    side = lax.rem(me, 2)
+    across = {"expert": place * 2 + 1 - side}
+    sibling = {"tensor": 1 - core}
+    along = [{"expert": flipped(place, k, experts) * 2 + side} for k in range(experts)]
+    rows = xa.shape[1]
+    cols = gate_ref.shape[2]
+
+    barrier = pltpu.get_barrier_semaphore()
+    for peer in [across, sibling] + along[1:]:
+        pl.semaphore_signal(barrier, inc=1, device_id=peer, device_id_type=MESH)
+
+    pairs = (
+        (gate_ref.at[0], lambda half: wg.at[:, pl.ds(half * cols, cols)]),
+        (up_ref.at[0], lambda half: wu.at[:, pl.ds(half * cols, cols)]),
+        (down_ref.at[0], lambda half: wd.at[pl.ds(half * cols, cols), :]),
+    )
+    loads = [
+        pltpu.make_async_copy(src, dst(0), load_sem.at[i]) for i, (src, dst) in enumerate(pairs)
+    ]
+    for load in loads:
+        load.start()
+
+    first = pl.multiple_of(core * rows, rows)
+    own = pl.ds(first, rows)
+    resident = tokens_ref[own, :].astype(jnp.float32)
+    inv_rms = lax.rsqrt(jnp.mean(resident * resident, axis=1, keepdims=True) + 1e-05)
+    xa[0] = (resident * inv_rms * gain_ref[...]).astype(jnp.bfloat16)
+
+    pl.semaphore_wait(barrier, experts + 1)
+
+    def remote(src, dst, send, recv, peer):
+        return pltpu.make_async_remote_copy(
+            src_ref=src, dst_ref=dst, send_sem=send, recv_sem=recv, device_id=peer,
+            device_id_type=MESH,
+        )
+
+    gather_z = [
+        remote(xa.at[0], xa.at[k], xa_send.at[k], xa_recv.at[k], along[k]) if k else None
+        for k in range(experts)
+    ]
+    gather_x = [
+        remote(xa.at[k], xb.at[k], xb_send.at[k], xb_recv.at[k], across) for k in range(experts)
+    ]
+    part_x = [
+        remote(x_send.at[k], x_recv.at[k], px_send.at[k], px_recv.at[k], across)
+        for k in range(experts)
+    ]
+    part_z = [
+        remote(z_send.at[k], z_recv.at[k], pz_send.at[k], pz_recv.at[k], along[k]) if k else None
+        for k in range(experts)
+    ]
+    swaps = [
+        remote(src, dst(1), swap_send.at[i], swap_recv.at[i], sibling)
+        for i, (src, dst) in enumerate(pairs)
+    ]
+
+    gather_x[0].start()
+    for k in range(1, experts):
+        gather_z[k].start()
+    for swap in swaps:
+        swap.start()
+
+    def close(k):
+        part_x[k].wait_recv()
+        both = own_out[k] + x_recv[k].astype(jnp.float32)
+        if k:
+            z_send[k] = both.astype(jnp.bfloat16)
+            part_z[k].start()
+        else:
+            own_out[0] = both
+
+    for k in range(experts):
+        if k + 1 < experts:
+            gather_z[k + 1].wait_recv()
+            gather_x[k + 1].start()
+        gather_x[k].wait_recv()
+        block = jnp.concatenate([xb[k], xa[k]], axis=0)
+        if k == 0:
+            loads[0].wait()
+            swaps[0].wait_recv()
+        gate_val = jnp.dot(block, wg[...], preferred_element_type=jnp.float32)
+        if k == 0:
+            loads[1].wait()
+            swaps[1].wait_recv()
+        up_val = jnp.dot(block, wu[...], preferred_element_type=jnp.float32)
+        hidden = gated_unit(gate_val, up_val).astype(jnp.bfloat16)
+        if k == 0:
+            loads[2].wait()
+            swaps[2].wait_recv()
+        result = jnp.dot(hidden, wd[...], preferred_element_type=jnp.float32)
+        x_send[k] = result[:rows].astype(jnp.bfloat16)
+        part_x[k].start()
+        own_out[k] = result[rows:]
+        if k:
+            close(k - 1)
+    close(experts - 1)
+
+    ids = ids_ref[own, :]
+    shares = weights_ref[own, :]
+    total = tokens_ref[own, :].astype(jnp.float32)
+    for k in range(experts):
+        expert = flipped(place, k, experts)
+        share = jnp.sum(jnp.where(ids == expert, shares, 0.0), axis=1, keepdims=True)
+        if k:
+            part_z[k].wait_recv()
+            value = z_recv[k].astype(jnp.float32)
+        else:
+            value = own_out[0]
+        total = total + share * value
+    final[...] = total.astype(jnp.bfloat16)
+    last = remote(final, out_ref.at[own, :], last_send, last_recv, sibling)
+    last.start()
+    out_ref[own, :] = final[...]
+
+    for k in range(experts):
+        gather_x[k].wait_send()
+        part_x[k].wait_send()
+        if k:
+            gather_z[k].wait_send()
+            part_z[k].wait_send()
+    for swap in swaps:
+        swap.wait_send()
+    last.wait_send()
+    last.wait_recv()
+
+
+def dense_layer(tokens, gain, route_ids, route_weights, w_gate, w_up, w_down):
+    experts = lax.axis_size("expert") // 2
+    features = tokens.shape[1]
+    rows = tokens.shape[0] // lax.axis_size("tensor")
+    units = 2 * w_gate.shape[2]
+    vmem = pl.BlockSpec(memory_space=pltpu.VMEM)
+    hbm = pl.BlockSpec(memory_space=pltpu.HBM)
+    half = jnp.bfloat16
+    dma = pltpu.SemaphoreType.DMA
+    slots = pltpu.VMEM((experts, rows, features), half)
+    return pl.pallas_call(
+        functools.partial(dense_kernel, experts),
+        out_shape=jax.ShapeDtypeStruct(tokens.shape, tokens.dtype),
+        in_specs=[vmem] * 4 + [hbm] * 3,
+        out_specs=vmem,
+        scratch_shapes=[
+            pltpu.VMEM((features, units), half),
+            pltpu.VMEM((features, units), half),
+            pltpu.VMEM((units, features), half),
+            slots,
+            slots,
+            pltpu.VMEM((experts, rows, features), jnp.float32),
+            slots,
+            slots,
+            slots,
+            slots,
+            pltpu.VMEM((rows, features), half),
+            dma((3,)),
+            dma((3,)),
+            dma((3,)),
+        ]
+        + [dma((experts,))] * 8
+        + [dma, dma],
+        compiler_params=pltpu.CompilerParams(
+            collective_id=0, has_side_effects=True, vmem_limit_bytes=48 * 1024 * 1024
+        ),
+    )(tokens, gain.reshape(1, features), route_ids, route_weights, w_gate, w_up, w_down)
 
 
 def route_tables(chosen_ids, chosen_weights, expert_count, slot_room):
@@ -28,7 +247,7 @@
     return (send_table, mix_table)
 
 
-def per_device(tokens, gain, route_ids, route_weights, w_gate, w_up, w_down):
+def routed_layer(tokens, gain, route_ids, route_weights, w_gate, w_up, w_down):
     expert_axis = lax.axis_size("expert")
     expert_count = expert_axis // 2
     tensor_count = lax.axis_size("tensor")
@@ -78,6 +297,18 @@
     return lax.all_gather(finished, "tensor", axis=0, tiled=True)
 
 
+def per_device(tokens, gain, route_ids, route_weights, w_gate, w_up, w_down):
+    experts = lax.axis_size("expert") // 2
+    dense = (
+        route_ids.shape[1] == experts
+        and experts & (experts - 1) == 0
+        and lax.axis_size("tensor") == 2
+        and w_gate.shape[0] == 1
+    )
+    layer = dense_layer if dense else routed_layer
+    return layer(tokens, gain, route_ids, route_weights, w_gate, w_up, w_down)
+
+
 def solution(mesh):
     placed = (
         P(("groups", "expert"), None),

time: 107 us -> 41.7 us (0.39)
  blocking collectives: 55.4 us -> 0 us
  Pallas kernels: 0 us -> 33.7 us
  waiting for transfers between devices: 21.5 us -> 0 us
  between operations: 13.5 us -> 0.01 us
  matrix products: 9.5 us -> 0 us
  local copies, waits for them, and re-layouts: 3.43 us -> 7.66 us
  other arithmetic: 2.86 us -> 0 us
    all_to_all x2 -> x0, blocking collectives: 53.5 us -> none  [the longest x1 27.3 us: per_device(): lax.all_to_all(outgoing, 'expert', split_axis=0, concat_axis=0, tiled=True)]
    pallas_call x0 -> x1, Pallas kernels: none -> 33.7 us  [dense_layer(): pl.pallas_call(functools.partial(dense_kernel, experts), out_shape=jax.Sh...]
    reduce_scatter x1 -> x0, waiting for transfers between devices: 12.5 us -> none  [per_device(): lax.psum_scatter(jnp.dot(hidden, down_local, preferred_element_type=jnp.f...]
    dot_general x5 -> x0, matrix products: 9.5 us -> none  [the longest x1 4.78 us: per_device(): jnp.dot(hidden, down_local, preferred_element_type=jnp.float32)]
    all_gather x1 -> x0, waiting for transfers between devices: 8.95 us -> none  [per_device(): row_piece = lax.all_gather(arrived, 'tensor', axis=0, tiled=True)]
    unnamed x8 -> x11, local copies, waits for them, and re-layouts: 1.57 us -> 6.96 us
    all_gather x1 -> x0, blocking collectives: 1.95 us -> none  [per_device(): return lax.all_gather(finished, 'tensor', axis=0, tiled=True)]
    dynamic_slice x2 -> x0, local copies, waits for them, and re-layouts: 1.52 us -> none  [the longest x1 0.76 us: per_device(): own_ids = lax.dynamic_slice_in_dim(route_ids, first_row, own_rows, 0)]
  transfers between devices with their start and end apart: 2 -> 0, of which waited for: 2 -> 0; matrix products, arithmetic and copies ran while one was open for 0% -> 0% of each run, Pallas kernels for 0% -> 0%
where the time goes in v1:
time: 41.7 us; the launch traced here: 41.3 us
  Pallas kernels  33.7 us (81%)
  local copies, waits for them, and re-layouts  7.66 us (18%)
    pallas_call x1, Pallas kernels, dense_layer(): pl.pallas_call(functools.partial(dense_kernel, experts), out_shape=jax.Sh...  33.7 us
    unnamed x11, local copies, waits for them, and re-layouts  6.96 us

profile of v1, /device:TPU:0, one launch (start us, length us, event | category | flops | bytes accessed | tf_op | source)
XLA Modules:
  0.0 41.3 jit_solution(9686498765019304560)
XLA Ops:
  0.0 0.7 %reshape.3.gain_ref = f32[1,1536]{1,0:T(1,128)S(1)} reshape(f32[1536]{0:T(1024)} %param.8) | data formatting | bytes 12288 | tf_op jit(solution)/shard_map/reshape | solution.py:227
  0.7 0.8 %copy.8.ids_ref = s32[64,4]{1,0:T(8,128)S(1)} copy(s32[64,4]{0,1:T(4,128)} %param.9) | data formatting | bytes 2048 | tf_op args[2]
  1.5 0.8 %copy.9.weights_ref = f32[64,4]{1,0:T(8,128)S(1)} copy(f32[64,4]{0,1:T(4,128)} %param.10) | data formatting | bytes 2048 | tf_op args[3]
  2.2 0.0 copy-start
  2.2 1.3 %copy-done = bf16[1,1536,384]{2,1,0:T(8,128)(2,1)S(1)} copy-done((bf16[1,1536,384]{2,1,0:T(8,128)(2,1)S(1)}, bf16[1,1536,384]{2,1,0:T(8,128)(2,1)}, u32[]{:S(2)}) %copy-start) | copy-done | bytes 1179672
  3.5 0.0 copy-start.1
  3.5 1.3 %copy-done.1 = bf16[1,1536,384]{2,1,0:T(8,128)(2,1)S(1)} copy-done((bf16[1,1536,384]{2,1,0:T(8,128)(2,1)S(1)}, bf16[1,1536,384]{2,1,0:T(8,128)(2,1)}, u32[]{:S(2)}) %copy-start.1) | copy-done | bytes 1179672
  4.8 0.0 copy-start.2
  4.8 1.3 %copy-done.2 = bf16[1,384,1536]{2,1,0:T(8,128)(2,1)S(1)} copy-done((bf16[1,384,1536]{2,1,0:T(8,128)(2,1)S(1)}, bf16[1,384,1536]{2,1,0:T(8,128)(2,1)}, u32[]{:S(2)}) %copy-start.2) | copy-done | bytes 1179672
  6.1 0.0 copy-start.3
  6.1 0.9 %copy-done.3 = bf16[64,1536]{1,0:T(8,128)(2,1)S(1)} copy-done((bf16[64,1536]{1,0:T(8,128)(2,1)S(1)}, bf16[64,1536]{1,0:T(8,128)(2,1)}, u32[]{:S(2)}) %copy-start.3) | copy-done | bytes 196632
  7.0 33.7 %shard_map.73 = bf16[64,1536]{1,0:T(8,128)(2,1)S(1)} custom-call(bf16[64,1536]{1,0:T(8,128)(2,1)S(1)} %copy-done.3, f32[1,1536]{1,0:T(1,128)S(1)} %reshape.3.gain_ref, s32[64,4]{1,0:T(8,128)S(1)} %copy.8.ids_ref, f32[64,4]{1,0:T(8,128)S(1)} %copy.9.weights_ref, bf16[1,1536,384]{2,1,0:T(8,128)(2,1)S(1)} %copy-done, bf16[1,1536,384]{2,1,0:T(8,128)(2,1)S(1)} %copy-done.1, ...), custom_call_target="tpu_custom_call" | custom-call | tf_op jit(solution)/shard_map/pallas_call | solution.py:201
  40.7 0.7 %copy.11 = bf16[64,1536]{1,0:T(8,128)(2,1)} copy(bf16[64,1536]{1,0:T(8,128)(2,1)S(1)} %shard_map.73) | data formatting | bytes 393216
Async XLA Ops:
  2.2 1.3 %copy-start = (bf16[1,1536,384]{2,1,0:T(8,128)(2,1)S(1)}, bf16[1,1536,384]{2,1,0:T(8,128)(2,1)}, u32[]{:S(2)}) copy-start(bf16[1,1536,384]{2,1,0:T(8,128)(2,1)} %gate_ref.1) | copy-start | bytes 3538948
  3.5 1.3 %copy-start.1 = (bf16[1,1536,384]{2,1,0:T(8,128)(2,1)S(1)}, bf16[1,1536,384]{2,1,0:T(8,128)(2,1)}, u32[]{:S(2)}) copy-start(bf16[1,1536,384]{2,1,0:T(8,128)(2,1)} %up_ref.1) | copy-start | bytes 3538948
  4.8 1.3 %copy-start.2 = (bf16[1,384,1536]{2,1,0:T(8,128)(2,1)S(1)}, bf16[1,384,1536]{2,1,0:T(8,128)(2,1)}, u32[]{:S(2)}) copy-start(bf16[1,384,1536]{2,1,0:T(8,128)(2,1)} %down_ref.1) | copy-start | bytes 3538948
  6.1 0.9 %copy-start.3 = (bf16[64,1536]{1,0:T(8,128)(2,1)S(1)}, bf16[64,1536]{1,0:T(8,128)(2,1)}, u32[]{:S(2)}) copy-start(bf16[64,1536]{1,0:T(8,128)(2,1)} %tokens_ref.1) | copy-start | bytes 589828

commit v2 on v1

--- a/solution.py
+++ b/solution.py
@@ -34,6 +34,10 @@
     up_ref,
     down_ref,
     out_ref,
+    held,
+    gain,
+    ids,
+    weights,
     wg,
     wu,
     wd,
@@ -45,6 +49,7 @@
     z_send,
     z_recv,
     final,
+    small_sem,
     load_sem,
     swap_send,
     swap_recv,
@@ -66,12 +71,27 @@
     across = {"expert": place * 2 + 1 - side}
     sibling = {"tensor": 1 - core}
     along = [{"expert": flipped(place, k, experts) * 2 + side} for k in range(experts)]
-    rows = xa.shape[1]
+    pieces, rows, width = xa.shape[1:]
     cols = gate_ref.shape[2]
+    own = pl.ds(pl.multiple_of(core * rows, rows), rows)
 
     barrier = pltpu.get_barrier_semaphore()
     for peer in [across, sibling] + along[1:]:
         pl.semaphore_signal(barrier, inc=1, device_id=peer, device_id_type=MESH)
+
+    smalls = [
+        pltpu.make_async_copy(src, dst, small_sem.at[i])
+        for i, (src, dst) in enumerate(
+            (
+                (tokens_ref.at[own, :], held),
+                (gain_ref, gain),
+                (ids_ref, ids),
+                (weights_ref, weights),
+            )
+        )
+    ]
+    for small in smalls:
+        small.start()
 
     pairs = (
         (gate_ref.at[0], lambda half: wg.at[:, pl.ds(half * cols, cols)]),
@@ -84,11 +104,16 @@
     for load in loads:
         load.start()
 
-    first = pl.multiple_of(core * rows, rows)
-    own = pl.ds(first, rows)
-    resident = tokens_ref[own, :].astype(jnp.float32)
+    def part(p):
+        return pl.ds(p * width, width)
+
+    smalls[0].wait()
+    resident = held[...].astype(jnp.float32)
     inv_rms = lax.rsqrt(jnp.mean(resident * resident, axis=1, keepdims=True) + 1e-05)
-    xa[0] = (resident * inv_rms * gain_ref[...]).astype(jnp.bfloat16)
+    smalls[1].wait()
+    normed = (resident * inv_rms * gain[...].reshape(1, -1)).astype(jnp.bfloat16)
+    for p in range(pieces):
+        xa[0, p] = normed[:, p * width : (p + 1) * width]
 
     pl.semaphore_wait(barrier, experts + 1)
 
@@ -98,94 +123,131 @@
             device_id_type=MESH,
         )
 
-    gather_z = [
-        remote(xa.at[0], xa.at[k], xa_send.at[k], xa_recv.at[k], along[k]) if k else None
-        for k in range(experts)
-    ]
-    gather_x = [
-        remote(xa.at[k], xb.at[k], xb_send.at[k], xb_recv.at[k], across) for k in range(experts)
-    ]
-    part_x = [
-        remote(x_send.at[k], x_recv.at[k], px_send.at[k], px_recv.at[k], across)
-        for k in range(experts)
-    ]
-    part_z = [
-        remote(z_send.at[k], z_recv.at[k], pz_send.at[k], pz_recv.at[k], along[k]) if k else None
-        for k in range(experts)
-    ]
+    def gather_z(k, p):
+        return remote(xa.at[0, p], xa.at[k, p], xa_send.at[k, p], xa_recv.at[k, p], along[k])
+
+    def gather_x(k, p):
+        return remote(xa.at[k, p], xb.at[k, p], xb_send.at[k, p], xb_recv.at[k, p], across)
+
+    def part_x(k, p):
+        return remote(
+            x_send.at[k, p], x_recv.at[k, p], px_send.at[k, p], px_recv.at[k, p], across
+        )
+
+    def part_z(k, p):
+        return remote(
+            z_send.at[k, p], z_recv.at[k, p], pz_send.at[k, p], pz_recv.at[k, p], along[k]
+        )
+
     swaps = [
         remote(src, dst(1), swap_send.at[i], swap_recv.at[i], sibling)
         for i, (src, dst) in enumerate(pairs)
     ]
 
-    gather_x[0].start()
-    for k in range(1, experts):
-        gather_z[k].start()
+    for p in range(pieces):
+        gather_x(0, p).start()
+        if experts > 1:
+            gather_z(1, p).start()
+    for k in range(2, experts):
+        for p in range(pieces):
+            gather_z(k, p).start()
     for swap in swaps:
         swap.start()
 
-    def close(k):
-        part_x[k].wait_recv()
-        both = own_out[k] + x_recv[k].astype(jnp.float32)
-        if k:
-            z_send[k] = both.astype(jnp.bfloat16)
-            part_z[k].start()
-        else:
-            own_out[0] = both
-
+    smalls[2].wait()
+    smalls[3].wait()
+    tokens_here = ids.shape[1]
+    row_at = lax.broadcasted_iota(jnp.int32, (rows, tokens_here), 0) + core * rows
+    on_row = row_at == lax.broadcasted_iota(jnp.int32, (rows, tokens_here), 1)
+    shares = []
     for k in range(experts):
-        if k + 1 < experts:
-            gather_z[k + 1].wait_recv()
-            gather_x[k + 1].start()
-        gather_x[k].wait_recv()
-        block = jnp.concatenate([xb[k], xa[k]], axis=0)
+        named = jnp.where(ids[...] == flipped(place, k, experts), weights[...], 0.0)
+        line = jnp.sum(named, axis=0, keepdims=True)
+        shares.append(jnp.sum(jnp.where(on_row, line, 0.0), axis=1, keepdims=True))
+
+    def forward(k):
+        for p in range(pieces):
+            gather_z(k, p).wait_recv()
+            gather_x(k, p).start()
+
+    def product(k, table):
+        value = None
+        for p in range(pieces):
+            block = jnp.concatenate([xb[k, p], xa[k, p]], axis=0)
+            term = jnp.dot(block, table[part(p), :], preferred_element_type=jnp.float32)
+            value = term if value is None else value + term
+        return value
+
+    def compute(k):
+        for p in range(pieces):
+            gather_x(k, p).wait_recv()
         if k == 0:
             loads[0].wait()
             swaps[0].wait_recv()
-        gate_val = jnp.dot(block, wg[...], preferred_element_type=jnp.float32)
+        gate_val = product(k, wg)
         if k == 0:
             loads[1].wait()
             swaps[1].wait_recv()
-        up_val = jnp.dot(block, wu[...], preferred_element_type=jnp.float32)
+        up_val = product(k, wu)
         hidden = gated_unit(gate_val, up_val).astype(jnp.bfloat16)
         if k == 0:
             loads[2].wait()
             swaps[2].wait_recv()
-        result = jnp.dot(hidden, wd[...], preferred_element_type=jnp.float32)
-        x_send[k] = result[:rows].astype(jnp.bfloat16)
-        part_x[k].start()
-        own_out[k] = result[rows:]
-        if k:
-            close(k - 1)
-    close(experts - 1)
-
-    ids = ids_ref[own, :]
-    shares = weights_ref[own, :]
-    total = tokens_ref[own, :].astype(jnp.float32)
+        for p in range(pieces):
+            result = jnp.dot(hidden, wd[:, part(p)], preferred_element_type=jnp.float32)
+            x_send[k, p] = result[:rows].astype(jnp.bfloat16)
+            if k:
+                part_x(k, p).start()
+            own_out[k, p] = result[rows:]
+
+    def close(k):
+        for p in range(pieces):
+            part_x(k, p).wait_recv()
+            both = own_out[k, p] + x_recv[k, p].astype(jnp.float32)
+            z_send[k, p] = both.astype(jnp.bfloat16)
+            part_z(k, p).start()
+
     for k in range(experts):
-        expert = flipped(place, k, experts)
-        share = jnp.sum(jnp.where(ids == expert, shares, 0.0), axis=1, keepdims=True)
-        if k:
-            part_z[k].wait_recv()
-            value = z_recv[k].astype(jnp.float32)
-        else:
-            value = own_out[0]
-        total = total + share * value
-    final[...] = total.astype(jnp.bfloat16)
-    last = remote(final, out_ref.at[own, :], last_send, last_recv, sibling)
-    last.start()
-    out_ref[own, :] = final[...]
-
-    for k in range(experts):
-        gather_x[k].wait_send()
-        part_x[k].wait_send()
-        if k:
-            gather_z[k].wait_send()
-            part_z[k].wait_send()
+        if k + 1 < experts:
+            forward(k + 1)
+        if k >= 3:
+            close(k - 2)
+        compute(k)
+    for p in range(pieces):
+        part_x(0, p).start()
+    for k in range(max(1, experts - 2), experts):
+        close(k)
+
+    for p in range(pieces):
+        part_x(0, p).wait_recv()
+        both = own_out[0, p] + x_recv[0, p].astype(jnp.float32)
+        own_out[0, p] = held[:, part(p)].astype(jnp.float32) + shares[0] * both
+    for p in range(pieces):
+        total = own_out[0, p]
+        for k in range(1, experts):
+            part_z(k, p).wait_recv()
+            total = total + shares[k] * z_recv[k, p].astype(jnp.float32)
+        final[:, part(p)] = total.astype(jnp.bfloat16)
+        remote(
+            final.at[:, part(p)], out_ref.at[own, part(p)], last_send.at[p], last_recv.at[p],
+            sibling,
+        ).start()
+        out_ref[own, part(p)] = total.astype(jnp.bfloat16)
+
+    for p in range(pieces):
+        for k in range(experts):
+            gather_x(k, p).wait_send()
+            part_x(k, p).wait_send()
+            if k:
+                gather_z(k, p).wait_send()
+                part_z(k, p).wait_send()
     for swap in swaps:
         swap.wait_send()
-    last.wait_send()
-    last.wait_recv()
+    for p in range(pieces):
+        remote(
+            final.at[:, part(p)], out_ref.at[own, part(p)], last_send.at[p], last_recv.at[p],
+            sibling,
+        ).wait()
 
 
 def dense_layer(tokens, gain, route_ids, route_weights, w_gate, w_up, w_down):
@@ -193,38 +255,46 @@
     features = tokens.shape[1]
     rows = tokens.shape[0] // lax.axis_size("tensor")
     units = 2 * w_gate.shape[2]
+    pieces = 2
     vmem = pl.BlockSpec(memory_space=pltpu.VMEM)
-    hbm = pl.BlockSpec(memory_space=pltpu.HBM)
+    hbm = pl.BlockSpec(memory_space=pl.ANY)
     half = jnp.bfloat16
     dma = pltpu.SemaphoreType.DMA
-    slots = pltpu.VMEM((experts, rows, features), half)
+    slots = pltpu.VMEM((experts, pieces, rows, features // pieces), half)
+    ids = route_ids.T
+    weights = route_weights.T
     return pl.pallas_call(
         functools.partial(dense_kernel, experts),
         out_shape=jax.ShapeDtypeStruct(tokens.shape, tokens.dtype),
-        in_specs=[vmem] * 4 + [hbm] * 3,
+        in_specs=[hbm] * 7,
         out_specs=vmem,
         scratch_shapes=[
+            pltpu.VMEM((rows, features), half),
+            pltpu.VMEM((features,), jnp.float32),
+            pltpu.VMEM(ids.shape, jnp.int32),
+            pltpu.VMEM(weights.shape, jnp.float32),
             pltpu.VMEM((features, units), half),
             pltpu.VMEM((features, units), half),
             pltpu.VMEM((units, features), half),
             slots,
             slots,
-            pltpu.VMEM((experts, rows, features), jnp.float32),
+            pltpu.VMEM((experts, pieces, rows, features // pieces), jnp.float32),
             slots,
             slots,
             slots,
             slots,
             pltpu.VMEM((rows, features), half),
+            dma((4,)),
             dma((3,)),
             dma((3,)),
             dma((3,)),
         ]
-        + [dma((experts,))] * 8
-        + [dma, dma],
+        + [dma((experts, pieces))] * 8
+        + [dma((pieces,))] * 2,
         compiler_params=pltpu.CompilerParams(
-            collective_id=0, has_side_effects=True, vmem_limit_bytes=48 * 1024 * 1024
+            collective_id=0, has_side_effects=True, vmem_limit_bytes=66_000_000
         ),
-    )(tokens, gain.reshape(1, features), route_ids, route_weights, w_gate, w_up, w_down)
+    )(tokens, gain, ids, weights, w_gate, w_up, w_down)
 
 
 def route_tables(chosen_ids, chosen_weights, expert_count, slot_room):

time: 41.7 us -> 34.2 us (0.82)
  local copies, waits for them, and re-layouts: 7.66 us -> 1.62 us
  Pallas kernels: 33.7 us -> 32.4 us
    unnamed x11 -> x1, local copies, waits for them, and re-layouts: 6.96 us -> 1.62 us
    pallas_call x1, Pallas kernels: 33.7 us -> 32.4 us  [dense_layer(): pl.pallas_call(functools.partial(dense_kernel, experts), out_shape=jax.Sh...]
    reshape x1 -> x0, local copies, waits for them, and re-layouts: 0.7 us -> none  [dense_layer(): gain.reshape(1, features)]
where the time goes in v2:
time: 34.2 us; the launch traced here: 34 us
  Pallas kernels  32.4 us (95%)
  local copies, waits for them, and re-layouts  1.62 us (5%)
    pallas_call x1, Pallas kernels, dense_layer(): pl.pallas_call(functools.partial(dense_kernel, experts), out_shape=jax.Sh...  32.4 us
    unnamed x1, local copies, waits for them, and re-layouts  1.62 us

profile of v2, /device:TPU:0, one launch (start us, length us, event | category | flops | bytes accessed | tf_op | source)
XLA Modules:
  0.0 34.0 jit_solution(7379100163584739713)
XLA Ops:
  0.0 32.4 %shard_map.73 = bf16[64,1536]{1,0:T(8,128)(2,1)} custom-call(bf16[64,1536]{1,0:T(8,128)(2,1)} %tokens_ref.1, f32[1536]{0:T(1024)} %gain_ref.1, s32[4,64]{1,0:T(4,128)} %bitcast.2, f32[4,64]{1,0:T(4,128)} %bitcast.3, bf16[1,1536,384]{2,1,0:T(8,128)(2,1)} %gate_ref.1, bf16[1,1536,384]{2,1,0:T(8,128)(2,1)} %up_ref.1, bf16[1,384,1536]{2,1,0:T(8,128)(2,1)} %down_ref.1), custom_call_target="tpu_custom_call" | custom-call | tf_op jit(solution)/shard_map/pallas_call | solution.py:266
  32.4 1.6 %copy.9 = bf16[64,1536]{1,0:T(8,128)(2,1)} copy(bf16[64,1536]{1,0:T(8,128)(2,1)} %shard_map.73) | data formatting | bytes 393216

commit v3 on v2

--- a/solution.py
+++ b/solution.py
@@ -63,6 +63,7 @@
     pz_recv,
     last_send,
     last_recv,
+    keep_sem,
 ):
     me = lax.axis_index("expert")
     core = lax.axis_index("tensor")
@@ -144,11 +145,12 @@
         for i, (src, dst) in enumerate(pairs)
     ]
 
+    order = list(range(experts))
     for p in range(pieces):
         gather_x(0, p).start()
-        if experts > 1:
-            gather_z(1, p).start()
-    for k in range(2, experts):
+        for k in order[1:2]:
+            gather_z(k, p).start()
+    for k in order[2:]:
         for p in range(pieces):
             gather_z(k, p).start()
     for swap in swaps:
@@ -207,16 +209,25 @@
             z_send[k, p] = both.astype(jnp.bfloat16)
             part_z(k, p).start()
 
-    for k in range(experts):
-        if k + 1 < experts:
-            forward(k + 1)
-        if k >= 3:
-            close(k - 2)
+    for step, k in enumerate(order):
+        if step + 1 < experts:
+            forward(order[step + 1])
+        if step >= 3:
+            close(order[step - 2])
         compute(k)
     for p in range(pieces):
         part_x(0, p).start()
-    for k in range(max(1, experts - 2), experts):
+    for k in order[max(1, experts - 2) :]:
         close(k)
+
+    def give(p):
+        there = out_ref.at[own, part(p)]
+        return remote(final.at[:, part(p)], there, last_send.at[p], last_recv.at[p], sibling)
+
+    def keep(p):
+        return pltpu.make_async_copy(
+            final.at[:, part(p)], out_ref.at[own, part(p)], keep_sem.at[p]
+        )
 
     for p in range(pieces):
         part_x(0, p).wait_recv()
@@ -224,15 +235,12 @@
         own_out[0, p] = held[:, part(p)].astype(jnp.float32) + shares[0] * both
     for p in range(pieces):
         total = own_out[0, p]
-        for k in range(1, experts):
+        for k in order[1:]:
             part_z(k, p).wait_recv()
             total = total + shares[k] * z_recv[k, p].astype(jnp.float32)
         final[:, part(p)] = total.astype(jnp.bfloat16)
-        remote(
-            final.at[:, part(p)], out_ref.at[own, part(p)], last_send.at[p], last_recv.at[p],
-            sibling,
-        ).start()
-        out_ref[own, part(p)] = total.astype(jnp.bfloat16)
+        give(p).start()
+        keep(p).start()
 
     for p in range(pieces):
         for k in range(experts):
@@ -244,10 +252,8 @@
     for swap in swaps:
         swap.wait_send()
     for p in range(pieces):
-        remote(
-            final.at[:, part(p)], out_ref.at[own, part(p)], last_send.at[p], last_recv.at[p],
-            sibling,
-        ).wait()
+        give(p).wait()
+        keep(p).wait()
 
 
 def dense_layer(tokens, gain, route_ids, route_weights, w_gate, w_up, w_down):
@@ -256,7 +262,6 @@
     rows = tokens.shape[0] // lax.axis_size("tensor")
     units = 2 * w_gate.shape[2]
     pieces = 2
-    vmem = pl.BlockSpec(memory_space=pltpu.VMEM)
     hbm = pl.BlockSpec(memory_space=pl.ANY)
     half = jnp.bfloat16
     dma = pltpu.SemaphoreType.DMA
@@ -267,7 +272,7 @@
         functools.partial(dense_kernel, experts),
         out_shape=jax.ShapeDtypeStruct(tokens.shape, tokens.dtype),
         in_specs=[hbm] * 7,
-        out_specs=vmem,
+        out_specs=hbm,
         scratch_shapes=[
             pltpu.VMEM((rows, features), half),
             pltpu.VMEM((features,), jnp.float32),
@@ -290,7 +295,7 @@
             dma((3,)),
         ]
         + [dma((experts, pieces))] * 8
-        + [dma((pieces,))] * 2,
+        + [dma((pieces,))] * 3,
         compiler_params=pltpu.CompilerParams(
             collective_id=0, has_side_effects=True, vmem_limit_bytes=66_000_000
         ),

time: 34.2 us -> 33.6 us (0.982)
  Pallas kernels: 32.4 us -> 31.9 us
    pallas_call x1, Pallas kernels: 32.4 us -> 31.9 us  [dense_layer(): pl.pallas_call(functools.partial(dense_kernel, experts), out_shape=jax.Sh...]
where the time goes in v3:
time: 33.6 us; the launch traced here: 33.5 us
  Pallas kernels  31.9 us (95%)
  local copies, waits for them, and re-layouts  1.62 us (5%)
    pallas_call x1, Pallas kernels, dense_layer(): pl.pallas_call(functools.partial(dense_kernel, experts), out_shape=jax.Sh...  31.9 us
    unnamed x1, local copies, waits for them, and re-layouts  1.62 us

profile of v3, /device:TPU:0, one launch (start us, length us, event | category | flops | bytes accessed | tf_op | source)
XLA Modules:
  0.0 33.5 jit_solution(485672344599027227)
XLA Ops:
  0.0 31.9 %shard_map.73 = bf16[64,1536]{1,0:T(8,128)(2,1)} custom-call(bf16[64,1536]{1,0:T(8,128)(2,1)} %tokens_ref.1, f32[1536]{0:T(1024)} %gain_ref.1, s32[4,64]{1,0:T(4,128)} %bitcast.2, f32[4,64]{1,0:T(4,128)} %bitcast.3, bf16[1,1536,384]{2,1,0:T(8,128)(2,1)} %gate_ref.1, bf16[1,1536,384]{2,1,0:T(8,128)(2,1)} %up_ref.1, bf16[1,384,1536]{2,1,0:T(8,128)(2,1)} %down_ref.1), custom_call_target="tpu_custom_call" | custom-call | tf_op jit(solution)/shard_map/pallas_call | solution.py:271
  31.9 1.6 %copy.9 = bf16[64,1536]{1,0:T(8,128)(2,1)} copy(bf16[64,1536]{1,0:T(8,128)(2,1)} %shard_map.73) | data formatting | bytes 393216
